TPU v7x, 256 devices: a whole 4x4x8 slice. The times are simulated.
256 devices in a mesh: fsdp: 8 (over y, core), sp: 32 (over z, x).
Axes of the slice: x: 4, y: 4, z: 8, core: 2. Of those that a mesh axis runs over, the one named last changes fastest.
Arguments:
- hidden: bfloat16 [8192, 8192], P('sp', 'fsdp'), may hold values from -23 to 23
- w_query: bfloat16 [8192, 4096], P('fsdp', 'sp'), may hold values from -0.125 to 0.125
- w_keyvalue: bfloat16 [8192, 1024], P('fsdp', 'sp'), may hold values from -0.125 to 0.125
- w_output: bfloat16 [4096, 8192], P('sp', 'fsdp'), may hold values from -0.375 to 0.375
- segment_ids: int32 [8192], P('sp'), may hold values from 0 to 7, never falling along the last dimension, each value on 1 to 2048 neighbouring positions
Outputs:
- attended: bfloat16 [8192, 8192], P('sp', 'fsdp')
Inputs may be any that keep to these rules, and one draw needn't show every extreme that they name: `segment_ids`: segment ids never fall along the sequence; every episode has between 1 and 2048 tokens.
All inputs are finite; a program needn't handle non-finite values.
Results may differ from a plain program's by a relative error of at most 0.0085.
The roundings to bfloat16 on the way count: a program that leaves them out, or rounds other values in their place, can miss the bound.
Values may be sent and summed in bfloat16 or wider, within the bound.
A program may use at most 128 MiB of HBM per device.

v0:
```python
import math

import jax
import jax.numpy as jnp
from jax import lax
from jax.sharding import Mesh
from jax.sharding import PartitionSpec as P

HD = 128
GROUP = 8
SP = ("sp_0", "sp_1")


ROPE_BASE = 500000.0
NEG_FILL = -1e30


def gather_axes(shard, axes, dim):
    for axis in reversed(axes):
        shard = lax.all_gather(shard, axis, axis=dim, tiled=True)
    return shard


def in_one_piece(arrays, axis, dim, along):
    both = jnp.concatenate(arrays, axis=along)
    whole, at, done = (lax.psum_scatter(both, axis, scatter_dimension=dim, tiled=True), 0, [])
    for a in arrays:
        done.append(lax.slice_in_dim(whole, at, at + a.shape[along], axis=along))
        at += a.shape[along]
    return tuple(done)


def joined_along(tiles, dim):
    tiles = jnp.moveaxis(tiles, 0, dim)
    dims = tiles.shape
    return tiles.reshape(*dims[:dim], dims[dim] * dims[dim + 1], *dims[dim + 2 :])


def copy_for_each(shard, axis):
    copies = jnp.broadcast_to(shard, (lax.axis_size(axis), *shard.shape))
    return lax.all_to_all(copies, axis, split_axis=0, concat_axis=0, tiled=True)


def gather_directly(shard, axis, dim):
    return joined_along(copy_for_each(shard, axis), dim)


def rotate(values, positions, head_count, width):
    row_count = values.shape[0]
    shaped = values.reshape(row_count, head_count, width)
    half_width = width // 2
    frequency = jnp.exp(
        jnp.arange(half_width, dtype=jnp.float32) * (-2.0 * math.log(ROPE_BASE) / width)
    )
    angles = positions.astype(jnp.float32)[:, None] * frequency[None, :]
    cosine = jnp.cos(angles)[:, None, :]
    sine_part = jnp.sin(angles)[:, None, :]
    lower_half = shaped[:, :, :half_width]
    upper_half = shaped[:, :, half_width:]
    turned = jnp.concatenate(
        [
            lower_half * cosine - upper_half * sine_part,
            upper_half * cosine + lower_half * sine_part,
        ],
        axis=2,
    )
    return turned.reshape(row_count, head_count * width)


def split_keys(kv_sum, positions, kv_count, width):
    row_count = kv_sum.shape[0]
    shaped = kv_sum.reshape(row_count, kv_count, 2, width)
    key_part = rotate(
        shaped[:, :, 0, :].reshape(row_count, kv_count * width), positions, kv_count, width
    )
    key_part = key_part.reshape(row_count, kv_count, 1, width)
    return jnp.concatenate([key_part, shaped[:, :, 1:2, :]], axis=2).astype(jnp.bfloat16)


def merge_keys(
    state_in, query_tile, query_pos_tile, query_seg_tile, key_tile, key_pos_tile, key_seg_tile
):
    running_max, running_sum, weighted = state_in
    allowed = (key_pos_tile[None, :] <= query_pos_tile[:, None]) & (
        key_seg_tile[None, :] == query_seg_tile[:, None]
    )
    key_part = key_tile[:, :HD]
    value_part = key_tile[:, HD:]
    scores = lax.dot_general(
        query_tile, key_part, (((1,), (1,)), ((), ())), preferred_element_type=jnp.float32
    ) * HD ** (-0.5)
    masked = jnp.where(allowed, scores, NEG_FILL)
    new_max = jnp.maximum(running_max, jnp.max(masked, axis=1))
    weights = jnp.where(allowed, jnp.exp(masked - new_max[:, None]), 0.0)
    new_sum = jnp.sum(weights, axis=1)
    new_weighted = jnp.dot(
        weights.astype(jnp.bfloat16), value_part, preferred_element_type=jnp.float32
    )
    return (new_max, new_sum, new_weighted)


def on_device(hidden, w_query, w_keyvalue, w_output, segment_ids):
    fsdp_count = lax.axis_size("fsdp")
    seq_count = lax.axis_size(SP)
    fsdp_index = lax.axis_index("fsdp")
    seq_index = lax.axis_index(SP)
    tok_rows = hidden.shape[0]
    sub_rows = tok_rows // fsdp_count
    kv_count = seq_count // GROUP
    query_rows = seq_count * sub_rows
    offsets = jnp.arange(query_rows, dtype=jnp.int32)
    query_pos = offsets // sub_rows * tok_rows + fsdp_index * sub_rows + offsets % sub_rows
    own_positions = (
        seq_index * tok_rows + fsdp_index * sub_rows + jnp.arange(sub_rows, dtype=jnp.int32)
    )

    def project(weight_block):
        return jnp.dot(hidden, weight_block, preferred_element_type=jnp.float32)

    query_part = project(lax.all_gather(w_query, SP, axis=1, tiled=True))
    kv_part = project(gather_axes(w_keyvalue, SP, 1))
    query_sum, kv_sum = in_one_piece((query_part, kv_part), "fsdp", 0, 1)
    query_local = rotate(query_sum, own_positions, seq_count, HD).astype(jnp.bfloat16)
    pairs = split_keys(kv_sum, own_positions, kv_count, HD)
    expanded = jnp.repeat(pairs, GROUP, axis=1).reshape(sub_rows, seq_count * 2 * HD)
    query_head, kv_head = (
        lax.all_to_all(query_local, SP, split_axis=1, concat_axis=0, tiled=True),
        lax.all_to_all(expanded, SP, split_axis=1, concat_axis=0, tiled=True),
    )
    segment_all = gather_directly(segment_ids, SP, 0)
    query_seg = segment_all[query_pos]
    initial = (
        jnp.full((query_rows,), NEG_FILL, jnp.float32),
        jnp.zeros((query_rows,), jnp.float32),
        jnp.zeros((query_rows, HD), jnp.float32),
    )
    block_keys = lax.all_gather(kv_head, "fsdp", axis=0, tiled=True)
    piece_rows = block_keys.shape[0]
    row_ids = jnp.arange(piece_rows, dtype=jnp.int32)
    source_id = row_ids // query_rows
    within = row_ids % query_rows
    key_pos = within // sub_rows * tok_rows + source_id * sub_rows + within % sub_rows
    key_seg = segment_all[key_pos]
    final_max, final_sum, final_weighted = merge_keys(
        initial, query_head, query_pos, query_seg, block_keys, key_pos, key_seg
    )
    attention = (final_weighted / final_sum[:, None]).astype(jnp.bfloat16)
    back_rows = lax.all_to_all(attention, SP, split_axis=0, concat_axis=1, tiled=True)
    mixed_rows = gather_directly(back_rows, "fsdp", 0)
    result = jnp.dot(
        mixed_rows,
        lax.all_gather(w_output, SP, axis=0, tiled=True),
        preferred_element_type=jnp.float32,
    )
    return result.astype(jnp.bfloat16)


def solution(mesh):
    split = Mesh(mesh.devices.reshape(mesh.shape["fsdp"], 8, 4), ("fsdp", "sp_0", "sp_1"))
    placed = (P(SP, "fsdp"), P("fsdp", SP), P("fsdp", SP), P(SP, "fsdp"), P(SP))
    return jax.shard_map(
        on_device, mesh=split, in_specs=placed, out_specs=P(SP, "fsdp"), check_vma=False
    )
```

profile of v0, /device:TPU:1, one launch (start us, length us, event | category | flops | bytes accessed | tf_op | source)
XLA Modules:
  0.0 430.6 jit_solution(3894006001487751051)
XLA Ops:
  6.5 0.0 copy-start
  6.5 0.0 all-gather.7.cloned.1.call-start
  6.5 12.5 %all_gather.16 = bf16[1024,128]{0,1:T(8,128)(2,1)} all-gather(bf16[1024,32]{0,1:T(8,128)(2,1)} %param.7), channel_id=1, replica_groups=mesh['fsdp'=8,'sp_0'=8,'sp_1'=4] {'sp_1'}, dimensions={1}, use_global_device_ids=true | all-gather | bytes 327680 | tf_op jit(solution)/shard_map/all_gather | solution.py:20
  19.1 0.0 all-gather.7.cloned.1.call-update
  19.1 0.0 all-gather.5.cloned.1.call-start
  19.1 0.7 all-gather.5.cloned.1.call-update
  19.8 0.0 reduce-scatter.2.cloned.1.call-start
  19.9 40.3 %all-gather.7.cloned.1.call-done = bf16[1024,1024]{0,1:T(8,128)(2,1)} async-done(((bf16[1024,128]{0,1:T(8,128)(2,1)}), bf16[1024,1024]{0,1:T(8,128)(2,1)}) %all-gather.7.cloned.1.call-update) | async-done | bytes 2097168 | tf_op jit(solution)/shard_map/all_gather | solution.py:20
  60.2 0.0 copy-done
  60.2 2.3 fusion.57
  62.6 101.9 %all-gather.5.cloned.1.call-done = bf16[1024,4096]{1,0:T(8,128)(2,1)} async-done(((bf16[1024,128]{1,0:T(8,128)(2,1)}), bf16[1024,4096]{1,0:T(8,128)(2,1)}) %all-gather.5.cloned.1.call-update) | async-done | bytes 8388624 | tf_op jit(solution)/shard_map/all_gather | solution.py:120
  164.5 5.7 %fusion.56 = f32[256,4096]{1,0:T(8,128)S(1)} fusion(bf16[256,1024]{1,0:T(8,128)(2,1)S(1)} %copy-done, bf16[1024,4096]{1,0:T(8,128)(2,1)} %all-gather.5.cloned.1.call-done), kind=kOutput, calls=%fused_computation.102 | convolution fusion | flops 2147483648 | bytes 13107200 | tf_op jit(solution)/shard_map/dot_general | solution.py:118
  170.2 0.0 copy-start.2
  170.3 2.8 pad_maximum_fusion
  173.1 0.0 reduce-scatter.2.cloned.1.call-update
  173.1 0.0 all-gather.9.cloned.1.call-start
  173.2 0.1 multiply_cosine_fusion
  173.4 42.0 %reduce-scatter.2.cloned.1.call-done = f32[32,5120]{1,0:T(8,128)} async-done(((f32[256,5120]{1,0:T(8,128)}), f32[32,5120]{1,0:T(8,128)}) %reduce-scatter.2.cloned.1.call-update) | async-done | bytes 655376 | tf_op jit(solution)/shard_map/reduce_scatter | solution.py:26
  215.4 0.9 slice.48
  216.3 0.1 reshape.346
  216.5 0.1 slice.52
  216.6 0.1 subtract_convert_fusion.1
  216.7 0.1 maximum_bitcast_fusion
  216.8 0.1 copy.17
  216.8 0.5 broadcast_in_dim.15
  217.3 0.3 all_to_all.51
  217.6 22.8 %all_to_all.65 = bf16[32,32,256]{2,0,1:T(8,128)(2,1)} all-to-all(bf16[32,32,256]{2,0,1:T(8,128)(2,1)S(1)} %all_to_all.51), channel_id=1, replica_groups=mesh['fsdp'=8,'sp_0'=8,'sp_1'=4] {'sp_0','sp_1'}, dimensions={1} | all-to-all | bytes 1048576 | tf_op jit(solution)/shard_map/all_to_all | solution.py:128
  240.5 0.0 all-gather.9.cloned.1.call-update
  240.5 0.0 all-gather.11.cloned.1.call-start
  240.5 0.5 all-gather.11.cloned.1.call-update
  241.1 0.0 copy-done.2
  241.1 0.6 broadcast_in_dim.14
  241.7 6.1 %all-to-all-start = ((s32[32,1,256]{2,1,0:T(1,128)}), s32[32,1,256]{2,1,0:T(1,128)S(1)}, u32[]{:S(2)}, u32[]{:S(2)}) async-start(s32[32,1,256]{2,1,0:T(1,128)} %broadcast_in_dim.14), calls=%async_computation | async-start | bytes 65536 | tf_op jit(solution)/shard_map/all_to_all | solution.py:41
  247.8 0.1 compare_select_fusion
  247.9 1.1 slice_bitcast_fusion
  249.0 0.1 copy.24
  249.1 0.2 fusion.55
  249.3 0.6 subtract_convert_fusion
  250.0 0.9 pad_maximum_fusion.1
  250.8 5.6 %all-to-all-done = s32[32,1,256]{2,1,0:T(1,128)S(1)} async-done(((s32[32,1,256]{2,1,0:T(1,128)}), s32[32,1,256]{2,1,0:T(1,128)S(1)}, u32[]{:S(2)}, u32[]{:S(2)}) %all-to-all-start) | async-done | bytes 32800 | tf_op jit(solution)/shard_map/all_to_all | solution.py:41
  256.5 4.1 all-to-all-start.1
  260.6 6.2 %gather_fusion.1 = s32[1024]{0:T(1024)S(1)} fusion(s32[8192]{0:T(1024)S(1)} %bitcast.34, s32[1024]{0:T(1024)S(1)} %broadcast_clamp_fusion.1), kind=kCustom, calls=%fused_computation.1 | custom fusion | bytes 12288 | tf_op jit(solution)/shard_map/gather | solution.py:131
  266.7 45.5 %gather_fusion = s32[8192]{0:T(1024)S(1)} fusion(s32[8192]{0:T(1024)S(1)} %bitcast.35, s32[8192]{0:T(1024)S(1)} %broadcast_clamp_fusion), kind=kCustom, calls=%fused_computation | custom fusion | bytes 98304 | tf_op jit(solution)/shard_map/gather | solution.py:143
  312.3 0.0 all-to-all-done.1
  312.3 0.0 all-gather.9.cloned.1.call-done
  312.3 15.3 %fusion = (f32[1024]{0:T(1024)S(1)}, f32[1024,8192]{1,0:T(8,128)}) fusion(s32[8192]{0:T(1024)S(1)} %gather_fusion, s32[8192]{0:T(1024)S(1)} %fusion.27, s32[1024]{0:T(1024)S(1)} %gather_fusion.1, s32[1024]{0:T(1024)S(1)} %fusion.48, bf16[1024,128]{1,0:T(8,128)(2,1)S(1)} %bitcast.40, bf16[8192,256]{1,0:T(8,128)(2,1)} %all-gather.9.cloned.1.call-done), kind=kOutput, calls=%fused_computation.5 | convolution fusion | flops 2197814272 | bytes 35991552 | tf_op jit(solution)/shard_map/dot_general | solution.py:89
  327.6 0.0 copy-start.3
  327.6 17.4 %fusion.1 = f32[1024]{0:T(1024)S(1)} fusion(f32[1024,8192]{1,0:T(8,128)} %get-tuple-element.14, f32[1024]{0:T(1024)S(1)} %broadcast_maximum_fusion, s32[8192]{0:T(1024)S(1)} %gather_fusion, s32[8192]{0:T(1024)S(1)} %fusion.27, s32[1024]{0:T(1024)S(1)} %gather_fusion.1, s32[1024]{0:T(1024)S(1)} %fusion.48), kind=kLoop, calls=%fused_computation.6 | loop fusion | flops 67107840 | bytes 33636352 | tf_op jit(solution)/shard_map/reduce_sum | solution.py:95
  344.9 0.0 copy-done.3
  345.0 15.1 %fusion.13 = bf16[1024,128]{1,0:T(8,128)(2,1)S(1)} fusion(bf16[8192,256]{1,0:T(8,128)(2,1)S(1)} %copy-done.3, f32[1024,8192]{1,0:T(8,128)} %get-tuple-element.14, f32[1024]{0:T(1024)S(1)} %broadcast_maximum_fusion, s32[8192]{0:T(1024)S(1)} %gather_fusion, s32[8192]{0:T(1024)S(1)} %fusion.27, s32[1024]{0:T(1024)S(1)} %gather_fusion.1, s32[1024]{0:T(1024)S(1)} %fusion.48, ...), kind=kOutput, calls=%fused_computation.15 | convolution fusion | flops 2214854656 | bytes 35995648 | tf_op jit(solution)/shard_map/dot_general | solution.py:96
  360.0 20.1 %all_to_all.66 = bf16[32,32,128]{2,1,0:T(8,128)(2,1)S(1)} all-to-all(bf16[32,32,128]{2,1,0:T(8,128)(2,1)S(1)} %bitcast.41), channel_id=1, replica_groups=mesh['fsdp'=8,'sp_0'=8,'sp_1'=4] {'sp_0','sp_1'}, dimensions={0} | all-to-all | bytes 524288 | tf_op jit(solution)/shard_map/all_to_all | solution.py:148
  380.2 1.6 broadcast_in_dim.20
  381.8 9.6 %all-to-all-start.4 = ((bf16[8,32,4096]{2,1,0:T(8,128)(2,1)}), bf16[8,32,4096]{2,1,0:T(8,128)(2,1)S(1)}, u32[]{:S(2)}, u32[]{:S(2)}) async-start(bf16[8,32,4096]{2,1,0:T(8,128)(2,1)} %broadcast_in_dim.20), calls=%async_computation.5 | async-start | bytes 4194304 | tf_op jit(solution)/shard_map/all_to_all | solution.py:41
  391.3 0.0 all-gather.11.cloned.1.call-done
  391.3 26.2 %all-to-all-done.4 = bf16[8,32,4096]{2,1,0:T(8,128)(2,1)S(1)} async-done(((bf16[8,32,4096]{2,1,0:T(8,128)(2,1)}), bf16[8,32,4096]{2,1,0:T(8,128)(2,1)S(1)}, u32[]{:S(2)}, u32[]{:S(2)}) %all-to-all-start.4) | async-done | bytes 2097184 | tf_op jit(solution)/shard_map/all_to_all | solution.py:41
  417.5 0.0 copy-start.1
  417.5 6.6 %convolution_convert_fusion = bf16[256,1024]{1,0:T(8,128)(2,1)} fusion(bf16[256,4096]{1,0:T(8,128)(2,1)S(1)} %bitcast.37, bf16[4096,1024]{1,0:T(8,128)(2,1)} %all-gather.11.cloned.1.call-done), kind=kOutput, calls=%fused_computation.13 | convolution fusion | flops 2147745792 | bytes 11010048 | tf_op jit(solution)/shard_map/dot_general | solution.py:150
  424.1 0.0 copy-done.1
  (13 shorter events, 0.2 us)
Async XLA Ops:
  6.5 53.7 %copy-start = (bf16[256,1024]{1,0:T(8,128)(2,1)S(1)}, bf16[256,1024]{1,0:T(8,128)(2,1)}, u32[]{:S(2)}) copy-start(bf16[256,1024]{1,0:T(8,128)(2,1)} %param.5) | copy-start | bytes 1572868
  6.5 53.7 %all-gather.7.cloned.1.call-start = ((), (), s32[]{:S(2)}) async-start(), calls=%async_computation.7 | async-start | bytes 2359296 | tf_op jit(solution)/shard_map/all_gather | solution.py:20
  19.1 145.4 %all-gather.5.cloned.1.call-start = ((), (), s32[]{:S(2)}) async-start(), calls=%async_computation.6 | async-start | bytes 8650752 | tf_op jit(solution)/shard_map/all_gather | solution.py:120
  19.8 195.5 %reduce-scatter.2.cloned.1.call-start = ((), (), s32[]{:S(2)}) async-start(), calls=%async_computation.8 | async-start | bytes 5898240 | tf_op jit(solution)/shard_map/reduce_scatter | solution.py:26
  170.2 70.8 %copy-start.2 = (s32[256]{0:T(256)S(1)}, s32[256]{0:T(256)}, u32[]{:S(2)}) copy-start(s32[256]{0:T(256)} %param.9) | copy-start | bytes 3076
  173.1 139.2 %all-gather.9.cloned.1.call-start = ((), (), s32[]{:S(2)}) async-start(), calls=%async_computation.9 | async-start | bytes 4718592 | tf_op jit(solution)/shard_map/all_gather | solution.py:137
  240.5 150.9 %all-gather.11.cloned.1.call-start = ((), (), s32[]{:S(2)}) async-start(), calls=%async_computation.10 | async-start | bytes 8650752 | tf_op jit(solution)/shard_map/all_gather | solution.py:152
  241.7 14.8 %all-to-all-start = ((s32[32,1,256]{2,1,0:T(1,128)}), s32[32,1,256]{2,1,0:T(1,128)S(1)}, u32[]{:S(2)}, u32[]{:S(2)}) async-start(s32[32,1,256]{2,1,0:T(1,128)} %broadcast_in_dim.14), calls=%async_computation | async-start | bytes 65536 | tf_op jit(solution)/shard_map/all_to_all | solution.py:41
  256.5 55.8 %all-to-all-start.1 = ((bf16[32,32,128]{2,0,1:T(8,128)(2,1)}), bf16[32,32,128]{2,0,1:T(8,128)(2,1)S(1)}, u32[]{:S(2)}, u32[]{:S(2)}) async-start(bf16[32,32,128]{2,0,1:T(8,128)(2,1)} %pad_maximum_fusion.1), calls=%async_computation.2 | async-start | bytes 524288 | tf_op jit(solution)/shard_map/all_to_all | solution.py:127
  327.6 17.4 %copy-start.3 = (bf16[8192,256]{1,0:T(8,128)(2,1)S(1)}, bf16[8192,256]{1,0:T(8,128)(2,1)}, u32[]{:S(2)}) copy-start(bf16[8192,256]{1,0:T(8,128)(2,1)} %all-gather.9.cloned.1.call-done) | copy-start | bytes 12582916
  381.8 35.8 %all-to-all-start.4 = ((bf16[8,32,4096]{2,1,0:T(8,128)(2,1)}), bf16[8,32,4096]{2,1,0:T(8,128)(2,1)S(1)}, u32[]{:S(2)}, u32[]{:S(2)}) async-start(bf16[8,32,4096]{2,1,0:T(8,128)(2,1)} %broadcast_in_dim.20), calls=%async_computation.5 | async-start | bytes 4194304 | tf_op jit(solution)/shard_map/all_to_all | solution.py:41
  417.5 6.6 %copy-start.1 = (bf16[256,1024]{1,0:T(8,128)(2,1)S(1)}, bf16[256,1024]{1,0:T(8,128)(2,1)}, u32[]{:S(2)}) copy-start(bf16[256,1024]{1,0:T(8,128)(2,1)} %param.5) | copy-start | bytes 1572868
Sparse Core Ops, SparseCore 0:
  19.2 40.9 all-gather.6
  62.7 101.7 all-gather.4
  173.2 42.0 reduce-scatter.1
  240.6 35.3 all-gather.8
  278.4 97.7 all-gather.10
where the time goes:
time: 431 us
  waiting for transfers between devices  217 us (50%)
  local copies, waits for them, and re-layouts  57.3 us (13%)
  blocking collectives  55.5 us (13%)
  matrix products  45 us (10%)
  other arithmetic  22.2 us (5%)
  starting transfers between devices  19.8 us (5%)
  between operations  13.4 us (3%)
    all_gather x1, waiting for transfers between devices, on_device(): query_part = project(lax.all_gather(w_query, SP, axis=1, tiled=True))  102 us
    gather x1, local copies, waits for them, and re-layouts, on_device(): key_seg = segment_all[key_pos]  45.5 us
    reduce_scatter x1, waiting for transfers between devices, in_one_piece(): lax.psum_scatter(both, axis, scatter_dimension=dim, tiled=True)  42 us
    all_gather x1, waiting for transfers between devices, gather_axes(): shard = lax.all_gather(shard, axis, axis=dim, tiled=True)  40.3 us
    all_to_all x2, waiting for transfers between devices, copy_for_each(): return lax.all_to_all(copies, axis, split_axis=0, concat_axis=0, tiled=True)  31.8 us
    all_to_all x1, blocking collectives, on_device(): lax.all_to_all(expanded, SP, split_axis=1, concat_axis=0, tiled=True)  22.8 us
    all_to_all x1, blocking collectives, on_device(): lax.all_to_all(attention, SP, split_axis=0, concat_axis=1, tiled=True)  20.1 us
    reduce_sum x1, other arithmetic, merge_keys(): new_sum = jnp.sum(weights, axis=1)  17.4 us
  transfers between devices with their start and end apart: 8, of which 5 were waited for; matrix products, arithmetic and copies ran while one was open for 25% of the time, Pallas kernels for 0%

commit v1 on v0

v1 whole, which is shorter than its diff:
```python
import functools
import math

import jax
import jax.numpy as jnp
import numpy as np
from jax import lax
from jax.experimental import pallas as pl
from jax.experimental.pallas import tpu as pltpu
from jax.sharding import Mesh
from jax.sharding import PartitionSpec as P

HD = 128
HALF = HD // 2
ROPE_BASE = 500000.0
NEG_FILL = -1e30
SEGMENTS = 8
CODES = 32000.0
MESH = pl.DeviceIdType.MESH
F32 = jnp.float32
BF16 = jnp.bfloat16


def dot(a, b):
    return lax.dot_general(a, b, (((1,), (0,)), ((), ())), preferred_element_type=F32)


def dot_nt(a, b):
    return lax.dot_general(a, b, (((1,), (1,)), ((), ())), preferred_element_type=F32)


def kernel(
    dims,
    h_hbm, wq_hbm, wk_hbm, wo_hbm, seg_hbm, freq_hbm, out,
    h, wk, seg, freq, hb, wb, wob, wk2, kvw, pq, rq, pk, rk, sq, yq, acc_q, sk, yk, sk_unit, yk_unit, sq_unit, yq_unit, acc_k,
    seg_win, cos_q, sin_q, qs, mix, send_part, recv_part, relay_out, relay_in, acc_o,
    sem_local, h_s, h_r, sw_s, sw_r, w_s, wk_s, w_r, wo_s, wo_r, d_s, d_r, dk_s, dk_r,
    yq_s, yq_r, yk_s, yk_r, yu_s, yu_r, sg_s, sg_r, kz_s, kz_r, kx_s, kx_r, kc_s, kc_r,
    my_s, my_r, mc_s, mc_r, xr_s, xr_r, xf_s, xf_r,
):
    ny, nz, tb, kd, nc = dims
    nx = 4
    zh = nz // 2
    block = nx * tb
    th = tb // 2
    x = lax.axis_index("x")
    y = lax.axis_index("y")
    z = lax.axis_index("z")
    c = lax.axis_index("c")
    named = jax.named_scope

    def x_at(d):
        return {"x": lax.rem(x + d + nx, nx)}

    def z_at(d):
        return {"z": lax.rem(z + d + nz, nz)}

    def y_at(d):
        return {"y": lax.rem(y + d + ny, ny)}

    partner = {"c": 1 - c}

    def rc(src, dst, ssem, rsem, dev):
        return pltpu.make_async_remote_copy(
            src_ref=src, dst_ref=dst, send_sem=ssem, recv_sem=rsem, device_id=dev, device_id_type=MESH
        )

    def go(cp):
        cp.start()
        return cp

    def whole(ref, ssem, rsem):
        return rc(ref, ref, ssem, rsem, {"c": 1 - c})

    hi = lax.div(x, 2)
    lanes = (pl.ds(0, HD), pl.ds(HD, HD))
    own_lanes = pl.ds(pl.multiple_of(2 * block + x * tb, tb), tb)
    own_rows = pl.ds(pl.multiple_of(z * HD, HD), HD)
    local = {
        "wk": pltpu.make_async_copy(wk_hbm, wk, sem_local.at[0]),
        "wk_own": pltpu.make_async_copy(wk_hbm.at[hi], wk2.at[0, hi], sem_local.at[1]),
        "wq": pltpu.make_async_copy(wq_hbm, wb.at[0, :, lanes[0]], sem_local.at[2]),
        "h": pltpu.make_async_copy(h_hbm, h, sem_local.at[3]),
        "seg": pltpu.make_async_copy(seg_hbm, seg, sem_local.at[4]),
        "seg_own": pltpu.make_async_copy(seg_hbm, seg_win.at[:, own_lanes], sem_local.at[5]),
        "freq": pltpu.make_async_copy(freq_hbm, freq, sem_local.at[6]),
        "wo": pltpu.make_async_copy(wo_hbm, wob.at[own_rows, :], sem_local.at[7]),
    }
    for cp in local.values():
        cp.start()

    barrier = pltpu.get_barrier_semaphore()
    greet = [x_at(d) for d in range(1, nx)] + [z_at(1), z_at(-1), z_at(2), z_at(-2), partner]
    greet += [y_at(d) for d in range(1, ny)]
    for dev in greet:
        pl.semaphore_signal(barrier, inc=1, device_id=dev, device_id_type=MESH)
    for name in ("wk", "wq", "h"):
        local[name].wait()
    with named("barrier"):
        pl.semaphore_wait(barrier, len(greet))

    swap = go(rc(wk.at[1 - hi], wk2.at[0, hi], sw_s, sw_r, x_at(2)))

    k_rows = (pl.ds(0, kd // 2), pl.ds(kd // 2, kd // 2))

    def w_copy(r, way, piece):
        rows = k_rows[piece]
        dst = wb.at[0, rows, lanes[1]] if r == zh else wb.at[r, rows, lanes[1 - way]]
        src = wb.at[0, rows, lanes[0]] if r == 1 else wb.at[r - 1, rows, lanes[1 - way]]
        return rc(src, dst, w_s, w_r.at[r - 1, way, piece], z_at(1 - 2 * way))

    def k_copy(r, way):
        part = pl.ds(0, 2)
        if r == zh:
            part = pl.ds(way, 1)
            dst = wk2.at[zh, part]
        else:
            dst = wk2.at[nz - r if way == 0 else r, part]
        src_at = 0 if r == 1 else (nz - r + 1 if way == 0 else r - 1)
        src = wk2.at[src_at, part]
        return rc(src, dst, wk_s, w_r.at[r - 1, way, 2], z_at(1 - 2 * way))

    def pieces(r, way):
        return (way,) if r == zh else (0, 1)

    w_cp = {}

    def k_step(r):
        for way in range(2):
            w_cp[r, way, 2].wait_recv()
            if r < zh:
                w_cp[r + 1, way, 2] = go(k_copy(r + 1, way))

    def w_step(r, piece):
        for way in range(2):
            if piece in pieces(r, way):
                w_cp[r, way, piece].wait_recv()
                if r < zh and piece in pieces(r + 1, way):
                    w_cp[r + 1, way, piece] = go(w_copy(r + 1, way, piece))

    h_rows = (pl.ds(0, th), pl.ds(th, th))
    for way in range(2):
        w_cp[1, way, 0] = go(w_copy(1, way, 0))
    for k in range(2):
        go(rc(h.at[h_rows[k]], hb.at[2, h_rows[k]], h_s, h_r.at[0, k], x_at(1)))
        go(rc(h.at[h_rows[1 - k]], hb.at[0, h_rows[1 - k]], h_s, h_r.at[1, k], x_at(-1)))

    local["seg"].wait()
    local["seg_own"].wait()
    local["freq"].wait()
    local["wk_own"].wait()

    def seg_x(d):
        return rc(seg, seg_win.at[:, own_lanes], sg_s, sg_r.at[0], x_at(d))

    for d in range(1, nx):
        go(seg_x(d))

    def blk(b):
        return pl.ds((2 - b) * block, block)

    def seg_z(b):
        return rc(seg_win.at[:, blk(0)], seg_win.at[:, blk(b)], sg_s, sg_r.at[1], z_at(b))

    row = lax.broadcasted_iota(jnp.int32, (block, HD), 0)
    pos = (z * block + row).astype(F32)
    angle = pos * freq[4 * 16:4 * 16 + 1, :]
    with named("swap"):
        swap.wait_recv()
    for way in range(2):
        w_cp[1, way, 2] = go(k_copy(1, way))
    for way in range(2):
        w_cp[1, way, 1] = go(w_copy(1, way, 1))
    with named("cos"):
        cos_q[...] = jnp.cos(angle)
    lane = lax.broadcasted_iota(jnp.int32, (block, HD), 1)
    with named("sin"):
        sin_q[...] = jnp.sin(angle) * jnp.where(lane < HALF, -1.0, 1.0)

    def h_recv(way, k):
        rows = h_rows[k] if way == 0 else h_rows[1 - k]
        return rc(h.at[rows], hb.at[2 if way == 0 else 0, rows], h_s, h_r.at[way, k], x_at(1))

    def fwd_hidden(k):
        h_recv(0, k).wait_recv()
        h_recv(1, k).wait_recv()
        if k == 0:
            go(rc(hb.at[2, h_rows[0]], hb.at[1, h_rows[0]], h_s, h_r.at[2, 0], x_at(1)))
            go(rc(hb.at[0, h_rows[1]], hb.at[1, h_rows[1]], h_s, h_r.at[2, 1], x_at(-1)))

    parity = lax.rem(z + c, 2)

    def sub(j):
        return h[...] if j == 0 else hb[j - 1]

    def rows_of(j):
        return pl.ds(pl.multiple_of(lax.rem(x + j, nx) * tb, tb), tb)

    order = (0, 1, 3, 2)
    parts = (pl.ds(0, 3), pl.ds(3, 1))

    def exchange(u, half):
        at = (slice(None), slice(None), lanes[half])
        return rc(pq.at[(u, *at)], rq.at[(u // 2, *at)], d_s, d_r.at[u // 2, half], partner)

    def project(u, js, halves=(0, 1)):
        at = pl.ds(halves[0] * HD, len(halves) * HD)
        for j in js:
            pq[u, order.index(j), :, at] = dot(sub(j), wb[u, :, at])

    def hand_over(u, halves=(0, 1)):
        @pl.when(parity != u % 2)
        def _():
            for half in halves:
                exchange(u, half).start()

    def y_copy(slot, dest):
        return rc(sq.at[slot], yq.at[slot], yq_s, yq_r, {"y": dest})

    def q_unit_y(slot, dest):
        return rc(sq_unit.at[slot], yq_unit.at[slot], yu_s.at[1], yu_r.at[1], {"y": dest})

    def deliver(u, halves=(0, 1)):
        @pl.when(parity == u % 2)
        def _():
            for half in halves:
                exchange(u, half).wait_recv()
                d = (u if half == 0 else (nz - u)) if u else (0 if half == 0 else zh)
                dest = lax.div(lax.rem(z + d, nz), 2)
                slot = lax.rem(y - dest + ny, ny) - 1

                @pl.when(dest == y)
                def _():
                    acc_q[...] = pq[u, :, :, lanes[half]] + rq[u // 2, :, :, lanes[half]]

                @pl.when(dest != y)
                def _():
                    total = pq[u, :, :, lanes[half]] + rq[u // 2, :, :, lanes[half]]
                    largest = jnp.maximum(jnp.max(jnp.abs(total), keepdims=True), 1e-33)
                    sq_unit[slot] = jnp.broadcast_to(largest.reshape(1, 1) * (1.0 / CODES), (8, HD))
                    q_unit_y(slot, dest).start()
                    sq[slot] = jnp.round(total * (CODES / largest)).astype(jnp.int32).astype(jnp.int16)
                    y_copy(slot, dest).start()

    rows_k = nz * 2 * 16

    def k_project(js):
        wk_all = wk2[...].reshape(rows_k, kd)
        for j in js:
            pk[:, order.index(j)] = dot_nt(wk_all, sub(j)).reshape(nz, 2, 16, tb)

    turns = (1, 3, 2, 0)

    def k_chunk(turn, core):
        return lax.rem(2 * lax.rem(y + turn, ny) + core - z + nz, nz)

    def k_exchange(turn, p):
        return rc(
            pk.at[k_chunk(turn, 1 - c), parts[p]], rk.at[turn, parts[p]], dk_s, dk_r.at[turn, p], partner
        )

    def k_hand_over(p):
        for turn in turns:
            k_exchange(turn, p).start()

    def k_copy_y(slot, p, dest):
        return rc(sk.at[slot, parts[p]], yk.at[slot, parts[p]], yk_s, yk_r, {"y": dest})

    def k_unit_y(slot, p, dest):
        return rc(sk_unit.at[slot, p], yk_unit.at[slot, p], yu_s.at[0], yu_r.at[0], {"y": dest})

    def k_deliver(p):
        for turn in turns:
            k_exchange(turn, p).wait_recv()
            dest = lax.rem(y + turn, ny)
            slot = ny - turn - 1
            total = pk[k_chunk(turn, c), parts[p]] + rk[turn, parts[p]]
            if turn == 0:
                acc_k[parts[p]] = total
            else:
                largest = jnp.maximum(jnp.max(jnp.abs(total), keepdims=True), 1e-33)
                sk_unit[slot, p] = jnp.broadcast_to(largest.reshape(1, 1) * (1.0 / CODES), (8, HD))
                k_unit_y(slot, p, dest).start()
                sk[slot, parts[p]] = jnp.round(total * (CODES / largest)).astype(jnp.int32).astype(jnp.int16)
                k_copy_y(slot, p, dest).start()

    def y_other():
        return lax.rem(y + 1, ny)

    o_cols = nc // 2

    def o_copy(r, way, piece):
        owner = lax.rem(z + (nz - r + 1 if way == 0 else r - 1), nz)
        at = wob.at[pl.ds(pl.multiple_of(owner * HD, HD), HD), pl.ds(piece * o_cols, o_cols)]
        return rc(at, at, wo_s, wo_r.at[r - 1, way, piece], z_at(1 - 2 * way))

    def o_step(r, piece, ways=(0, 1)):
        for way in ways:
            if r == 0:
                go(o_copy(1, way, piece))
            elif r < zh or way == 1:
                o_copy(r, way, piece).wait_recv()
                if r + 1 < zh or (r + 1 == zh and way == 1):
                    go(o_copy(r + 1, way, piece))

    early = (0, 1, 3)
    with named("k1"):
        k_step(1)
    with named("w1a"):
        w_step(1, 0)
    with named("hidden0"):
        fwd_hidden(0)
    with named("k2"):
        k_step(2)
    with named("w1b"):
        w_step(1, 1)
    with named("hidden1"):
        fwd_hidden(1)
    with named("project0a"):
        project(0, early, (0,))
    with named("k3"):
        if zh > 3:
            k_step(3)
    with named("w2a"):
        w_step(2, 0)
    with named("project1a"):
        project(1, early)
    whole(seg_win.at[:, pl.ds(0, 3 * tb)], sg_s, sg_r.at[0]).wait_recv()
    for b in (1, 2):
        go(seg_z(b))
    with named("w2b"):
        w_step(2, 1)
    with named("k4"):
        k_step(zh)
    with named("kproject_a"):
        k_project(early)
        k_hand_over(0)
    with named("hidden2"):
        for k in range(2):
            rc(h.at[h_rows[k]], hb.at[1, h_rows[k]], h_s, h_r.at[2, k], x_at(1)).wait_recv()
    with named("kproject_b"):
        k_project((2,))
        k_hand_over(1)
    with named("project1b"):
        project(1, (2,))
        hand_over(1)
    with named("kdeliver_a"):
        k_deliver(0)
    with named("project0b"):
        project(0, (2,), (0,))
        hand_over(0, (0,))
    with named("w3a"):
        w_step(3, 0)
    with named("kdeliver_b"):
        k_deliver(1)
    with named("w3b"):
        if zh > 3:
            w_step(3, 1)
    local["wo"].wait()
    o_step(0, 0)
    o_step(0, 1, (1,))
    with named("project2"):
        project(2, range(nx))
        hand_over(2)
    with named("project3"):
        if zh > 3:
            project(3, range(nx))
            hand_over(3)
    place = 2 * lax.rem(x, 2) + hi
    k_freq = freq[pl.ds(pl.multiple_of(place * 16, 16), 16), 0:1]
    is_key = c == 0
    tables = []
    for j in order:
        first = z * block + lax.rem(x + j, nx) * tb
        k_angle = (first + lax.broadcasted_iota(jnp.int32, (16, tb), 1)).astype(F32) * k_freq
        tables.append((jnp.where(is_key, jnp.cos(k_angle), 1.0), jnp.where(is_key, jnp.sin(k_angle), 0.0)))

    whole(seg_win.at[:, pl.ds(0, 2 * block)], sg_s, sg_r.at[1]).wait_recv()

    wpos = lax.broadcasted_iota(jnp.int32, (1, 3 * block), 1)
    ids = jnp.where(wpos + (z - 2) * block >= 0, seg_win[...], -1)
    starts = [jnp.sum((ids < s).astype(F32), axis=1, keepdims=True).astype(jnp.int32) for s in range(SEGMENTS)]
    with named("deliver10"):
        deliver(1)
        deliver(0, (0,))
    with named("deliver2"):
        deliver(2)
    with named("deliver3"):
        if zh > 3:
            deliver(3)
    with named("ywait_k"):
        whole(yk_unit, yu_s.at[0], yu_r.at[0]).wait_recv()
        whole(yk, yk_s, yk_r).wait_recv()
    for e, j in enumerate(order):
        total = acc_k[e]
        for s in range(ny - 1):
            unit_of = yk_unit[s, 0 if e < 3 else 1][0:1, 0:1].reshape(1, 1, 1)
            total = total + yk[s, e].astype(jnp.int32).astype(F32) * unit_of
        low, high = total[0], total[1]
        cos_e, sin_e = tables[e]
        there = pl.ds(pl.multiple_of(2 * block + lax.rem(x + j, nx) * tb, tb), tb)
        kvw[c, 0, place, :, there] = (low * cos_e - high * sin_e).astype(BF16)
        kvw[c, 1, place, :, there] = (high * cos_e + low * sin_e).astype(BF16)

    def kz(b):
        return rc(kvw.at[c, :, place, :, blk(0)], kvw.at[c, :, place, :, blk(b)], kz_s, kz_r.at[b - 1], z_at(b))

    def kx(b, d):
        at = kvw.at[c, :, place, :, blk(b)]
        return rc(at, at, kx_s, kx_r.at[b], x_at(d))

    def kx_wait(b):
        whole(kvw.at[c, :, pl.ds(0, nx - 1), :, blk(b)], kx_s, kx_r.at[b]).wait_recv()

    def kc(b):
        at = kvw.at[c, :, :, :, blk(b)]
        return rc(at, at, kc_s, kc_r.at[b], partner)

    for b in (1, 2):
        go(kz(b))
    for d in range(1, nx):
        go(kx(0, d))
    o_step(0, 1, (0,))

    with named("w4"):
        for piece in range(2):
            w_step(zh, piece)
    with named("project0c"):
        project(0, range(nx), (1,))
        hand_over(0, (1,))
    with named("deliver0"):
        deliver(0, (1,))
    with named("kz1"):
        kz(1).wait_recv()
    for d in range(1, nx):
        go(kx(1, d))
    with named("o1a"):
        o_step(1, 0)
    with named("kz2"):
        kz(2).wait_recv()
    for d in range(1, nx):
        go(kx(2, d))
    with named("o1b-"):
        o_step(1, 1, (1,))
    with named("kx0"):
        kx_wait(0)
    go(kc(0))
    with named("o2a-"):
        o_step(2, 0, (1,))
    with named("kx1"):
        kx_wait(1)
    go(kc(1))
    with named("o1b+"):
        o_step(1, 1, (0,))
    with named("kx2"):
        kx_wait(2)
    go(kc(2))
    with named("o2b-"):
        o_step(2, 1, (1,))

    with named("ywait_q"):
        whole(yq_unit, yu_s.at[1], yu_r.at[1]).wait_recv()
        whole(yq, yq_s, yq_r).wait_recv()
    with named("rope"):
        for e, j in enumerate(order):
            q = acc_q[e]
            for s in range(ny - 1):
                q = q + yq[s, e].astype(jnp.int32).astype(F32) * yq_unit[s][0:1, 0:1]
            qs[e] = (q * cos_q[rows_of(j)] + pltpu.roll(q, HALF, 1) * sin_q[rows_of(j)]).astype(BF16)
    reach = 2 * block + tb
    unit = HD**-0.5 * math.log2(math.e)
    f = 2 * y + c
    own_f = pl.ds(pl.multiple_of(f * HD, HD), HD)
    with named("kcwait"):
        for b in (0, 1, 2):
            kc(b).wait_recv()

    def attend(j):
        t = lax.rem(x + j, nx)
        at = pl.multiple_of(t * tb, tb)
        q = qs[order.index(j)]
        keys = kvw[0, :, :, :, pl.ds(at, reach)].reshape(HD, reach)
        values = kvw[1, :, :, :, pl.ds(at, reach)].reshape(HD, reach)
        scores = dot(q, keys) * unit
        here = lax.broadcasted_iota(jnp.int32, (tb, 1), 0) + 2 * block
        begin = jnp.zeros((tb, 1), jnp.int32)
        for s in starts:
            begin = jnp.maximum(begin, jnp.where(s - at <= here, s - at, 0))
        k_at = lax.broadcasted_iota(jnp.int32, (tb, reach), 1)
        ahead, own = slice(0, 2 * block), slice(2 * block, reach)
        scores = jnp.concatenate(
            [
                jnp.where(k_at[:, ahead] >= begin, scores[:, ahead], NEG_FILL),
                jnp.where((k_at[:, own] >= begin) & (k_at[:, own] <= here), scores[:, own], NEG_FILL),
            ],
            axis=1,
        )
        top = jnp.max(scores, axis=1, keepdims=True)
        weights = jnp.exp2(scores - top)
        total = jnp.sum(weights, axis=1, keepdims=True)
        mixed = dot_nt(weights.astype(BF16), values)
        mix[j, :, own_f] = (mixed / total).astype(BF16)
        for d in range(1, ny):
            go(my(j, d))
        go(mc(j, 0))

    def my(j, d):
        at = mix.at[j, :, own_f]
        return rc(at, at, my_s, my_r.at[j, d - 1], y_at(d))

    def mc(j, d):
        fd = 2 * lax.rem(y - d + ny, ny) + c
        at = mix.at[j, :, pl.ds(pl.multiple_of(fd * HD, HD), HD)]
        return rc(at, at, mc_s, mc_r.at[j], partner)

    def pass_mix(j):
        for d in range(1, ny):
            my(j, d).wait_recv()
            go(mc(j, d))

    def have_mix(j):
        whole(mix.at[j, :, pl.ds(0, ny * HD)], mc_s, mc_r.at[j]).wait_recv()

    def half_of(k):
        return pl.ds(k * th, th)

    def cols(i):
        return pl.ds(i * o_cols, o_cols)

    def relay(k, i):
        return rc(relay_out.at[k, :, cols(i)], relay_in.at[k, :, cols(i)], xr_s, xr_r.at[k, i], x_at(1 - 2 * k))

    def final(k, part, i):
        at = (k, half_of(1 - k) if part == 0 else half_of(k), cols(i))
        return rc(send_part.at[at], recv_part.at[at], xf_s, xf_r.at[i], x_at(1 - 2 * k))

    def out_dot(j, k, i):
        return dot(mix[j, half_of(k)], wob[:, cols(i)])

    with named("att2"):
        attend(2)
    with named("o2a+"):
        o_step(2, 0, (0,))
    with named("o3a-"):
        o_step(3, 0, (1,))
    with named("att1"):
        attend(1)
    with named("o2b+"):
        o_step(2, 1, (0,))
    with named("o3b-"):
        o_step(3, 1, (1,))
    with named("att3"):
        attend(3)
    with named("gm2"):
        pass_mix(2)
    with named("o4a"):
        o_step(3, 0, (0,))
        o_step(zh, 0)
    with named("mix2"):
        have_mix(2)
    with named("mm2"):
        for k in range(2):
            relay_out[k, :, cols(0)] = out_dot(2, k, 0).astype(BF16)
            go(relay(k, 0))
    with named("o4b"):
        o_step(3, 1, (0,))
        o_step(zh, 1)
    with named("mm2"):
        for k in range(2):
            relay_out[k, :, cols(1)] = out_dot(2, k, 1).astype(BF16)
            go(relay(k, 1))
    with named("gm1"):
        pass_mix(1)
    with named("att0"):
        attend(0)
    with named("mm1"):
        have_mix(1)
        for i in range(2):
            send_part[0, half_of(1), cols(i)] = out_dot(1, 1, i).astype(BF16)
            go(final(0, 0, i))
    with named("gm3"):
        pass_mix(3)
        have_mix(3)
    with named("mm3"):
        for i in range(2):
            send_part[1, half_of(0), cols(i)] = out_dot(3, 0, i).astype(BF16)
            go(final(1, 0, i))
    with named("mm31"):
        for i in range(2):
            for k, j in ((0, 1), (1, 3)):
                acc_o[k, :, cols(i)] = out_dot(j, k, i)
        pass_mix(0)
    for i in range(2):
        for k in range(2):
            with named("relay"):
                relay(k, i).wait_recv()
            send_part[k, half_of(k), cols(i)] = (acc_o[k, :, cols(i)] + relay_in[k, :, cols(i)].astype(F32)).astype(BF16)
            go(final(k, 1, i))
    with named("mm0"):
        have_mix(0)
        for i in range(2):
            for k in range(2):
                acc_o[k, :, cols(i)] = out_dot(0, k, i)

    with named("drain"):
        for ref, ssem, rsem in (
            (hb, h_s, h_r.at[0, 0]),
            (wk.at[0], sw_s, sw_r),
            (wb.at[:, pl.ds(0, kd - kd // 8)], w_s, w_r.at[0, 0, 0]),
            (wk2.at[pl.ds(0, nz - 1)], wk_s, w_r.at[0, 0, 0]),
            (wob.at[pl.ds(0, (nz - 1) * HD)], wo_s, wo_r.at[0, 0, 0]),
            (rq, d_s, d_r.at[0, 0]),
            (rk, dk_s, dk_r.at[0, 0]),
            (yq, yq_s, yq_r),
            (seg_win.at[:, pl.ds(0, 3 * tb + 2 * block)], sg_s, sg_r.at[0]),
            (kvw.at[0, :, pl.ds(0, 2), :, blk(0)], kz_s, kz_r.at[0]),
            (kvw.at[0, :, pl.ds(0, 3)], kx_s, kx_r.at[0]),
            (kvw.at[0], kc_s, kc_r.at[0]),
            (mix.at[pl.ds(0, 3), half_of(0)], my_s, my_r.at[0, 0]),
            (mix.at[pl.ds(0, 2)], mc_s, mc_r.at[0]),
            (relay_out, xr_s, xr_r.at[0, 0]),
            (send_part, xf_s, xf_r.at[0]),
        ):
            whole(ref, ssem, rsem).wait_send()

        whole(yk, yk_s, yk_r).wait_send()
        whole(yk_unit, yu_s.at[0], yu_r.at[0]).wait_send()
        whole(yq_unit, yu_s.at[1], yu_r.at[1]).wait_send()
    for i in range(2):
        with named("final"):
            whole(recv_part.at[:, :, cols(i)], xf_s, xf_r.at[i]).wait_recv()
        for k in range(2):
            rows = half_of(k)
            out[rows, cols(i)] = (
                acc_o[k, :, cols(i)] + recv_part[0, rows, cols(i)].astype(F32) + recv_part[1, rows, cols(i)].astype(F32)
            ).astype(BF16)


def on_device(ny, nz, hidden, w_query, w_keyvalue, w_output, segment_ids):
    tb, kd = hidden.shape
    nc = w_output.shape[1]
    nx, zh, block, th = 4, nz // 2, 4 * hidden.shape[0], hidden.shape[0] // 2
    freq = np.exp(np.arange(HALF, dtype=np.float32) * np.float32(-2.0 * math.log(ROPE_BASE) / HD))
    table = np.zeros((72, HD), np.float32)
    table[:HALF, 0] = freq
    table[HALF] = np.concatenate([freq, freq])
    dma = pltpu.SemaphoreType.DMA
    vm = pltpu.VMEM
    scratch = [
        vm((tb, kd), BF16),
        vm((2, 16, kd), BF16),
        vm((1, tb), jnp.int32),
        vm((72, HD), F32),
        vm((3, tb, kd), BF16),
        vm((zh, kd, 2 * HD), BF16),
        vm((nz * HD, nc), BF16),
        vm((nz, 2, 16, kd), BF16),
        vm((2, 2, 4, 16, 3 * block), BF16),
        vm((zh, nx, tb, 2 * HD), F32),
        vm((zh // 2, nx, tb, 2 * HD), F32),
        vm((nz, nx, 2, 16, tb), F32),
        vm((nz // 2, nx, 2, 16, tb), F32),
        vm((ny - 1, nx, tb, HD), jnp.int16),
        vm((ny - 1, nx, tb, HD), jnp.int16),
        vm((nx, tb, HD), F32),
        vm((ny - 1, nx, 2, 16, tb), jnp.int16),
        vm((ny - 1, nx, 2, 16, tb), jnp.int16),
        vm((ny - 1, 2, 8, HD), F32),
        vm((ny - 1, 2, 8, HD), F32),
        vm((ny - 1, 8, HD), F32),
        vm((ny - 1, 8, HD), F32),
        vm((nx, 2, 16, tb), F32),
        vm((1, 3 * block), jnp.int32),
        vm((block, HD), F32),
        vm((block, HD), F32),
        vm((nx, tb, HD), BF16),
        vm((nx, tb, nz * HD), BF16),
        vm((2, tb, nc), BF16),
        vm((2, tb, nc), BF16),
        vm((2, th, nc), BF16),
        vm((2, th, nc), BF16),
        vm((2, th, nc), F32),
        dma((8,)),
        dma, dma((3, 2)),
        dma, dma,
        dma, dma, dma((zh, 2, 3)),
        dma, dma((zh, 2, 2)),
        dma, dma((zh // 2, 2)),
        dma, dma((ny, 2)),
        dma, dma,
        dma, dma,
        dma((2,)), dma((2,)),
        dma, dma((2,)),
        dma, dma((2,)),
        dma, dma((3,)),
        dma, dma((3,)),
        dma, dma((nx, ny - 1)),
        dma, dma((nx,)),
        dma, dma((2, 2)),
        dma, dma((2,)),
    ]
    anywhere = pl.BlockSpec(memory_space=pl.ANY)
    return pl.pallas_call(
        functools.partial(kernel, (ny, nz, tb, kd, nc)),
        out_shape=pltpu.VMEM((tb, nc), BF16),
        in_specs=[anywhere] * 6,
        out_specs=pl.BlockSpec(memory_space=pltpu.VMEM),
        scratch_shapes=scratch,
        compiler_params=pltpu.CompilerParams(
            collective_id=0, has_side_effects=True, vmem_limit_bytes=60 * 2**20
        ),
    )(
        hidden,
        w_query,
        w_keyvalue.T.reshape(2, 16, kd),
        w_output,
        segment_ids.reshape(1, tb),
        jnp.asarray(table),
    )


def solution(mesh):
    ny, nz = mesh.shape["fsdp"] // 2, mesh.shape["sp"] // 4
    split = Mesh(mesh.devices.reshape(ny, 2, nz, 4), ("y", "c", "z", "x"))
    rows, cols = ("z", "x"), ("y", "c")
    placed = (P(rows, cols), P(cols, rows), P(cols, rows), P(rows, cols), P(rows))
    return jax.shard_map(
        functools.partial(on_device, ny, nz),
        mesh=split,
        in_specs=placed,
        out_specs=P(rows, cols),
        check_vma=False,
    )
```

time: 431 us -> 82.6 us (0.19)
  waiting for transfers between devices: 217 us -> 0 us
  Pallas kernels: 0 us -> 81.7 us
  local copies, waits for them, and re-layouts: 57.3 us -> 0.8 us
  blocking collectives: 55.5 us -> 0 us
  matrix products: 45 us -> 0 us
  other arithmetic: 22.2 us -> 0 us
  starting transfers between devices: 19.8 us -> 0 us
  between operations: 13.4 us -> 0.01 us
    all_gather x4 -> x0, waiting for transfers between devices: 142 us -> none  [the longest x1 102 us: on_device(): query_part = project(lax.all_gather(w_query, SP, axis=1, tiled=True))]
    pallas_call x0 -> x1, Pallas kernels: none -> 81.7 us  [on_device(): pl.pallas_call(functools.partial(kernel, (ny, nz, tb, kd, nc)), out_shape...]
    gather x2 -> x0, local copies, waits for them, and re-layouts: 51.7 us -> none  [the longest x1 45.5 us: on_device(): key_seg = segment_all[key_pos]]
    dot_general x5 -> x0, matrix products: 45 us -> none  [the longest x1 15.3 us: merge_keys(): lax.dot_general(query_tile, key_part, (((1,), (1,)), ((), ())), preferred...]
    all_to_all x2 -> x0, blocking collectives: 42.9 us -> none  [the longest x1 22.8 us: on_device(): lax.all_to_all(expanded, SP, split_axis=1, concat_axis=0, tiled=True)]
    reduce_scatter x1 -> x0, waiting for transfers between devices: 42 us -> none  [in_one_piece(): lax.psum_scatter(both, axis, scatter_dimension=dim, tiled=True)]
    all_to_all x3 -> x0, waiting for transfers between devices: 31.9 us -> none  [the longest x2 31.8 us: copy_for_each(): return lax.all_to_all(copies, axis, split_axis=0, concat_axis=0, tiled=True)]
    all_to_all x3 -> x0, starting transfers between devices: 19.7 us -> none  [the longest x2 15.6 us: copy_for_each(): return lax.all_to_all(copies, axis, split_axis=0, concat_axis=0, tiled=True)]
  transfers between devices with their start and end apart: 8 -> 0, of which waited for: 5 -> 0; matrix products, arithmetic and copies ran while one was open for 25% -> 0% of each run, Pallas kernels for 0% -> 0%
where the time goes in v1:
time: 82.6 us; the launch traced here: 82.5 us
  Pallas kernels  81.7 us (99%)
    pallas_call x1, Pallas kernels, on_device(): pl.pallas_call(functools.partial(kernel, (ny, nz, tb, kd, nc)), out_shape...  81.7 us

profile of v1, /device:TPU:1, one launch (start us, length us, event | category | flops | bytes accessed | tf_op | source)
XLA Modules:
  0.0 82.5 jit_solution(4594983150429271137)
XLA Ops:
  0.0 81.7 %shard_map.64 = bf16[256,1024]{1,0:T(8,128)(2,1)S(1)} custom-call(bf16[256,1024]{1,0:T(8,128)(2,1)} %h_hbm.1, bf16[1024,128]{1,0:T(8,128)(2,1)} %wq_hbm.1, bf16[2,16,1024]{2,1,0:T(8,128)(2,1)} %bitcast.4, bf16[128,1024]{1,0:T(8,128)(2,1)} %wo_hbm.1, s32[1,256]{1,0:T(1,128)} %bitcast.5, f32[72,128]{1,0:T(8,128)} %constant.2.clone.freq_hbm), custom_call_target="tpu_custom_call" | custom-call | tf_op jit(solution)/shard_map/pallas_call | solution.py:703
  81.7 0.8 copy.8

commit v2 on v1

--- a/solution.py
+++ b/solution.py
@@ -475,18 +475,19 @@
         for b in (0, 1, 2):
             kc(b).wait_recv()
 
-    def attend(j):
+    def attend(j, rows=None):
+        first, count = (0, tb) if rows is None else (rows * th, th)
         t = lax.rem(x + j, nx)
         at = pl.multiple_of(t * tb, tb)
-        q = qs[order.index(j)]
+        q = qs[order.index(j), pl.ds(first, count)]
         keys = kvw[0, :, :, :, pl.ds(at, reach)].reshape(HD, reach)
         values = kvw[1, :, :, :, pl.ds(at, reach)].reshape(HD, reach)
         scores = dot(q, keys) * unit
-        here = lax.broadcasted_iota(jnp.int32, (tb, 1), 0) + 2 * block
-        begin = jnp.zeros((tb, 1), jnp.int32)
+        here = lax.broadcasted_iota(jnp.int32, (count, 1), 0) + (2 * block + first)
+        begin = jnp.zeros((count, 1), jnp.int32)
         for s in starts:
             begin = jnp.maximum(begin, jnp.where(s - at <= here, s - at, 0))
-        k_at = lax.broadcasted_iota(jnp.int32, (tb, reach), 1)
+        k_at = lax.broadcasted_iota(jnp.int32, (count, reach), 1)
         ahead, own = slice(0, 2 * block), slice(2 * block, reach)
         scores = jnp.concatenate(
             [
@@ -499,14 +500,15 @@
         weights = jnp.exp2(scores - top)
         total = jnp.sum(weights, axis=1, keepdims=True)
         mixed = dot_nt(weights.astype(BF16), values)
-        mix[j, :, own_f] = (mixed / total).astype(BF16)
+        mix[j, pl.ds(first, count), own_f] = (mixed / total).astype(BF16)
         for d in range(1, ny):
-            go(my(j, d))
-        go(mc(j, 0))
-
-    def my(j, d):
-        at = mix.at[j, :, own_f]
-        return rc(at, at, my_s, my_r.at[j, d - 1], y_at(d))
+            go(my(j, d, rows))
+        if rows != 0:
+            go(mc(j, 0))
+
+    def my(j, d, rows=None):
+        at = mix.at[j, :, own_f] if rows is None else mix.at[j, pl.ds(rows * th, th), own_f]
+        return rc(at, at, my_s, my_r.at[j if rows != 0 else nx, d - 1], y_at(d))
 
     def mc(j, d):
         fd = 2 * lax.rem(y - d + ny, ny) + c
@@ -515,7 +517,9 @@
 
     def pass_mix(j):
         for d in range(1, ny):
-            my(j, d).wait_recv()
+            if j == 2:
+                my(j, d, 0).wait_recv()
+            my(j, d, 1 if j == 2 else None).wait_recv()
             go(mc(j, d))
 
     def have_mix(j):
@@ -538,7 +542,8 @@
         return dot(mix[j, half_of(k)], wob[:, cols(i)])
 
     with named("att2"):
-        attend(2)
+        attend(2, 0)
+        attend(2, 1)
     with named("o2a+"):
         o_step(2, 0, (0,))
     with named("o3a-"):
@@ -694,7 +699,7 @@
         dma, dma((2,)),
         dma, dma((3,)),
         dma, dma((3,)),
-        dma, dma((nx, ny - 1)),
+        dma, dma((nx + 1, ny - 1)),
         dma, dma((nx,)),
         dma, dma((2, 2)),
         dma, dma((2,)),

time: 82.6 us -> 82.1 us (level)
  no operation moved by 1% of the time
where the time goes in v2:
time: 82.1 us; the launch traced here: 82 us
  Pallas kernels  81.2 us (99%)
    pallas_call x1, Pallas kernels, on_device(): pl.pallas_call(functools.partial(kernel, (ny, nz, tb, kd, nc)), out_shape...  81.2 us

profile of v2, /device:TPU:1, one launch (start us, length us, event | category | flops | bytes accessed | tf_op | source)
XLA Modules:
  0.0 82.0 jit_solution(4914067454711532164)
XLA Ops:
  0.0 81.2 %shard_map.64 = bf16[256,1024]{1,0:T(8,128)(2,1)S(1)} custom-call(bf16[256,1024]{1,0:T(8,128)(2,1)} %h_hbm.1, bf16[1024,128]{1,0:T(8,128)(2,1)} %wq_hbm.1, bf16[2,16,1024]{2,1,0:T(8,128)(2,1)} %bitcast.4, bf16[128,1024]{1,0:T(8,128)(2,1)} %wo_hbm.1, s32[1,256]{1,0:T(1,128)} %bitcast.5, f32[72,128]{1,0:T(8,128)} %constant.2.clone.freq_hbm), custom_call_target="tpu_custom_call" | custom-call | tf_op jit(solution)/shard_map/pallas_call | solution.py:708
  81.2 0.8 copy.8
